TPU v7x, 32 devices: a whole 2x2x4 slice. The times are simulated.
32 devices in a mesh: site: 2 (over y), handler: 4 (over x, core), worker: 4 (over z).
Axes of the slice: x: 2, y: 2, z: 4, core: 2. Of those that a mesh axis runs over, the one named last changes fastest.
Arguments:
- sgt: bfloat16 [2048, 6, 3, 1024], P(('site', 'handler', 'worker')), parts along dimension 0, may hold values from -6 to 6
- mechanism: bfloat16 [6, 1024], P(None, ('handler', 'worker')), may hold values from -2.5 to 2.5
- req_owner: int32 [1024, 1], P(('site', 'handler', 'worker')), parts along dimension 0, may hold values from 0 to 15; in each aligned block of 32 rows (0 to 31, 32 to 63, ...) at most 4 rows name the same one
- req_local: int32 [1024], P(('site', 'handler', 'worker')), parts along dimension 0, may hold values from 0 to 31
- slip: bfloat16 [1024, 64, 128], P(('site', 'handler', 'worker')), parts along dimension 0, may hold values from 0 to 0.029907227
Outputs:
- seismograms: float32 [32, 64, 3, 1024], P(('site', 'handler'), 'worker'), parts along dimension 0
There are 2 independent parts, one for each index of `site`. A program takes and returns all parts, laid end to end along the dimension named above; an argument that names none is the same for every part. Nothing has to cross between parts.
Inputs may be any that keep to these rules, and one draw needn't show every extreme that they name: `req_owner`: among the 32 requests of one device no owner is named more than 4 times, and in every draw some device names some owner exactly 4 times; every owner is named somewhere.
All inputs are finite; a program needn't handle non-finite values.
Results may differ from a plain program's by a relative error of at most 0.0029.
Values may be sent and summed in bfloat16 or wider, within the bound.
A program may use at most 128 MiB of HBM per device.

v0:
```python
import jax
import jax.numpy as jnp
from jax import lax
from jax.sharding import PartitionSpec as P

TAPS = 64
BLK = 2
RUP_SLOTS = 4


def combine_points(sgt, mechanism):
    total = mechanism[0].astype(jnp.float32)[:, None, None] * sgt[:, 0].astype(jnp.float32)
    for comp in range(1, 6):
        total = total + mechanism[comp].astype(jnp.float32)[:, None, None] * sgt[:, comp].astype(
            jnp.float32
        )
    return total.astype(jnp.bfloat16)


def shifted_blocks(green):
    samples = green.shape[-1]
    padded = jnp.pad(green, ((0, 0), (0, 0), (0, 0), (TAPS, 0)))
    return jnp.stack(
        [padded[..., TAPS - lag : TAPS - lag + samples] for lag in range(TAPS)], axis=2
    )


def deliver(first, second):
    return (
        lax.all_to_all(first, ("handler", "worker"), split_axis=0, concat_axis=0, tiled=True),
        lax.all_to_all(second, ("handler", "worker"), split_axis=0, concat_axis=0, tiled=True),
    )


def local(sgt, mechanism, req_owner, req_local, slip):
    peers = lax.axis_size(("handler", "worker"))
    samples = sgt.shape[-1]
    blocks_here = sgt.shape[0] // BLK
    requests = req_local.shape[0]
    capacity = max(2, (2 * requests + peers - 1) // peers)
    owner = req_owner[:, 0]
    member = (owner[:, None] == jnp.arange(peers, dtype=jnp.int32)[None, :]).astype(jnp.int32)
    earlier = jnp.sum((jnp.cumsum(member, axis=0) - member) * member, axis=1)
    position = owner * capacity + earlier
    table = jnp.full((peers * capacity,), -1, jnp.int32).at[position].set(req_local)
    asked = lax.all_to_all(
        table.reshape(peers, capacity),
        ("handler", "worker"),
        split_axis=0,
        concat_axis=0,
        tiled=True,
    )
    wanted = (asked >= 0).reshape(-1)
    picked = jnp.where(wanted, asked.reshape(-1), 0)
    green_here = combine_points(sgt, mechanism).reshape(blocks_here, BLK, 3, samples)
    chosen = jnp.where(wanted[:, None, None, None], green_here[picked], jnp.zeros((), jnp.bfloat16))
    chosen = chosen.reshape(peers, capacity, BLK, 3, samples)
    front, back = deliver(chosen[:, :, :, :2], chosen[:, :, :, 2:])
    arrived = jnp.concatenate([front, back], axis=3)
    blocks = arrived.reshape(peers * capacity, BLK, 3, samples)[position]
    rows = requests // RUP_SLOTS
    variations = slip.shape[1]
    outputs = []
    for slot in range(RUP_SLOTS):
        stacked = shifted_blocks(blocks[slot * rows : (slot + 1) * rows])
        right = stacked.reshape(rows * BLK * TAPS, 3 * samples)
        left = jnp.transpose(slip[slot * rows : (slot + 1) * rows], (1, 0, 2)).reshape(
            variations, rows * BLK * TAPS
        )
        outputs.append(
            jnp.dot(left, right, preferred_element_type=jnp.float32).reshape(variations, 3, samples)
        )
    partial_value = jnp.stack(outputs, axis=0)
    return lax.psum_scatter(partial_value, "worker", scatter_dimension=1, tiled=True)


def solution(mesh):
    return jax.shard_map(
        local,
        mesh=mesh,
        in_specs=(
            P(("site", "handler", "worker"), None, None, None),
            P(None, ("handler", "worker")),
            P(("site", "handler", "worker"), None),
            P(("site", "handler", "worker")),
            P(("site", "handler", "worker"), None, None),
        ),
        out_specs=P(("site", "handler"), "worker", None, None),
        check_vma=False,
    )
```

profile of v0, /device:TPU:0, one launch (start us, length us, event | category | flops | bytes accessed | tf_op | source)
XLA Modules:
  0.0 499.9 jit_solution(5243394420854645857)
XLA Ops:
  7.3 0.8 select_reduce_fusion
  10.3 7.4 %all-to-all-start = ((s32[16,1,4]{2,1,0:T(1,128)}), s32[16,1,4]{2,1,0:T(1,128)S(1)}, u32[]{:S(2)}, u32[]{:S(2)}) async-start(s32[16,1,4]{2,1,0:T(1,128)} %bitcast.3), calls=%async_computation | async-start | bytes 16384 | tf_op jit(solution)/shard_map/all_to_all | solution.py:46
  17.7 3.6 slice_convert_fusion.5
  22.3 1.6 reshape.163
  23.9 2.5 reshape.165
  26.4 2.5 reshape.167
  28.9 2.5 reshape.169
  32.0 2.8 add_convert_fusion
  36.3 2.2 gather_fusion
  39.3 0.9 slice.1105
  40.2 6.0 %all-to-all-start.2 = ((bf16[16,4,2,1,1024]{4,2,3,1,0:T(2,128)(2,1)}), bf16[16,4,2,1,1024]{4,2,3,1,0:T(2,128)(2,1)S(1)}, u32[]{:S(2)}, u32[]{:S(2)}) async-start(bf16[16,4,2,1,1024]{4,2,3,1,0:T(2,128)(2,1)} %slice.1105), calls=%async_computation.2 | async-start | bytes 524288 | tf_op jit(solution)/shard_map/all_to_all | solution.py:31
  46.2 1.2 slice.1104
  47.4 8.6 %all-to-all-done.2 = bf16[16,4,2,1,1024]{4,2,3,1,0:T(2,128)(2,1)S(1)} async-done(((bf16[16,4,2,1,1024]{4,2,3,1,0:T(2,128)(2,1)}), bf16[16,4,2,1,1024]{4,2,3,1,0:T(2,128)(2,1)S(1)}, u32[]{:S(2)}, u32[]{:S(2)}) %all-to-all-start.2) | async-done | bytes 262176 | tf_op jit(solution)/shard_map/all_to_all | solution.py:31
  55.9 3.6 all-to-all-start.1
  59.9 1.8 slice_bitcast_fusion.3
  61.7 13.5 %all-to-all-done.1 = bf16[16,4,2,2,1024]{4,2,3,1,0:T(2,128)(2,1)S(1)} async-done(((bf16[16,4,2,2,1024]{4,2,3,1,0:T(2,128)(2,1)}), bf16[16,4,2,2,1024]{4,2,3,1,0:T(2,128)(2,1)S(1)}, u32[]{:S(2)}, u32[]{:S(2)}) %all-to-all-start.1) | async-done | bytes 524320 | tf_op jit(solution)/shard_map/all_to_all | solution.py:30
  75.1 1.0 pad_maximum_fusion.1
  76.2 1.3 gather_fusion.1
  77.8 1.0 constant_dynamic-update-slice_fusion.63
  78.8 1.0 constant_dynamic-update-slice_fusion.62
  89.5 0.8 constant_dynamic-update-slice_fusion.49
  112.2 0.8 constant_dynamic-update-slice_fusion.21
  121.1 1.2 constant_dynamic-update-slice_fusion.10
  130.4 9.5 %copy.112 = bf16[8,2,64,3,1024]{4,3,2,1,0:T(4,128)(2,1)} copy(bf16[8,2,64,3,1024]{4,1,3,0,2:T(2,128)(2,1)} %constant_dynamic-update-slice_fusion) | data formatting | bytes 12582912 | tf_op jit(solution)/shard_map/stack | solution.py:23
  139.9 7.5 %copy.126 = bf16[128,8,3,1024]{3,1,2,0:T(8,128)(2,1)S(1)} copy(bf16[128,8,3,1024]{3,2,1,0:T(4,128)(2,1)} %bitcast.599) | data formatting | bytes 12582912
  147.4 1.2 convolution_bitcast_fusion.3
  153.2 1.0 constant_dynamic-update-slice_fusion.120
  196.2 0.8 constant_dynamic-update-slice_fusion.67
  199.4 9.7 %copy.114 = bf16[8,2,64,3,1024]{4,3,2,1,0:T(4,128)(2,1)} copy(bf16[8,2,64,3,1024]{4,1,3,0,2:T(2,128)(2,1)} %constant_dynamic-update-slice_fusion.64) | data formatting | bytes 12582912 | tf_op jit(solution)/shard_map/stack | solution.py:23
  209.1 7.5 %copy.127 = bf16[128,8,3,1024]{3,1,2,0:T(8,128)(2,1)S(1)} copy(bf16[128,8,3,1024]{3,2,1,0:T(4,128)(2,1)} %bitcast.600) | data formatting | bytes 12582912
  216.6 1.2 convolution_bitcast_fusion.2
  218.4 1.0 constant_dynamic-update-slice_fusion.190
  239.6 0.8 constant_dynamic-update-slice_fusion.164
  240.5 1.3 constant_dynamic-update-slice_fusion.163
  270.0 9.5 %copy.116 = bf16[8,2,64,3,1024]{4,3,2,1,0:T(4,128)(2,1)} copy(bf16[8,2,64,3,1024]{4,1,3,0,2:T(2,128)(2,1)} %constant_dynamic-update-slice_fusion.128) | data formatting | bytes 12582912 | tf_op jit(solution)/shard_map/stack | solution.py:23
  279.5 7.6 %copy.128 = bf16[128,8,3,1024]{3,1,2,0:T(8,128)(2,1)S(1)} copy(bf16[128,8,3,1024]{3,2,1,0:T(4,128)(2,1)} %bitcast.601) | data formatting | bytes 12582912
  287.2 2.1 convolution_bitcast_fusion.1
  289.3 1.7 stack_reshape.14
  329.8 0.8 constant_dynamic-update-slice_fusion.205
  341.1 9.7 %copy.118 = bf16[8,2,64,3,1024]{4,3,2,1,0:T(4,128)(2,1)} copy(bf16[8,2,64,3,1024]{4,1,3,0,2:T(2,128)(2,1)} %constant_dynamic-update-slice_fusion.192) | data formatting | bytes 12582912 | tf_op jit(solution)/shard_map/stack | solution.py:23
  350.8 7.5 %copy.129 = bf16[128,8,3,1024]{3,1,2,0:T(8,128)(2,1)S(1)} copy(bf16[128,8,3,1024]{3,2,1,0:T(4,128)(2,1)} %bitcast.602) | data formatting | bytes 12582912
  358.4 2.1 convolution_bitcast_fusion
  360.5 2.5 stack_reshape.15
  363.0 2.4 pad_maximum_fusion
  365.4 4.7 copy.120
  371.3 118.8 %all-reduce.7.cloned.1.call-done = f32[4,64,3,1024]{3,0,2,1:T(4,128)} async-done(((f32[4,64,3,1024]{3,0,2,1:T(4,128)}), f32[4,64,3,1024]{3,0,2,1:T(4,128)}) %all-reduce.7.cloned.1.call-update) | async-done | bytes 3145744
  490.1 1.2 constant_dynamic-slice_fusion
  491.3 1.3 copy.121
  (277 shorter events, 202.9 us)
Async XLA Ops:
  10.3 24.5 %all-to-all-start = ((s32[16,1,4]{2,1,0:T(1,128)}), s32[16,1,4]{2,1,0:T(1,128)S(1)}, u32[]{:S(2)}, u32[]{:S(2)}) async-start(s32[16,1,4]{2,1,0:T(1,128)} %bitcast.3), calls=%async_computation | async-start | bytes 16384 | tf_op jit(solution)/shard_map/all_to_all | solution.py:46
  21.3 10.0 %copy-start.1 = (bf16[6,64]{1,0:T(8,128)(2,1)S(1)}, bf16[6,64]{1,0:T(8,128)(2,1)}, u32[]{:S(2)}) copy-start(bf16[6,64]{1,0:T(8,128)(2,1)} %param.6) | copy-start | bytes 2308
  40.2 15.8 %all-to-all-start.2 = ((bf16[16,4,2,1,1024]{4,2,3,1,0:T(2,128)(2,1)}), bf16[16,4,2,1,1024]{4,2,3,1,0:T(2,128)(2,1)S(1)}, u32[]{:S(2)}, u32[]{:S(2)}) async-start(bf16[16,4,2,1,1024]{4,2,3,1,0:T(2,128)(2,1)} %slice.1105), calls=%async_computation.2 | async-start | bytes 524288 | tf_op jit(solution)/shard_map/all_to_all | solution.py:31
  55.9 19.2 %all-to-all-start.1 = ((bf16[16,4,2,2,1024]{4,2,3,1,0:T(2,128)(2,1)}), bf16[16,4,2,2,1024]{4,2,3,1,0:T(2,128)(2,1)S(1)}, u32[]{:S(2)}, u32[]{:S(2)}) async-start(bf16[16,4,2,2,1024]{4,2,3,1,0:T(2,128)(2,1)} %slice.1104), calls=%async_computation.1 | async-start | bytes 1048576 | tf_op jit(solution)/shard_map/all_to_all | solution.py:30
  59.6 430.5 %all-reduce.7.cloned.1.call-start = ((), (), s32[]{:S(2)}) async-start(), calls=%async_computation.3 | async-start | bytes 6291456
  350.8 7.5 %copy-start = (bf16[8,8,8,128]{3,2,1,0:T(8,128)(2,1)S(1)}, bf16[8,8,8,128]{3,2,1,0:T(8,128)(2,1)}, u32[]{:S(2)}) copy-start(bf16[8,8,8,128]{3,2,1,0:T(8,128)(2,1)} %get-tuple-element.19) | copy-start | bytes 393220
  365.4 4.7 copy-start.2
Sparse Core Ops, SparseCore 0:
  370.2 119.8 all-reduce.6
where the time goes:
time: 507 us; the launch traced here: 500 us
  local copies, waits for them, and re-layouts  307 us (61%)
  waiting for transfers between devices  141 us (28%)
  starting transfers between devices  17.3 us (3%)
  between operations  14.9 us (3%)
  other arithmetic  13.6 us (3%)
  matrix products  6.58 us (1%)
    unnamed x260, local copies, waits for them, and re-layouts  235 us
    unnamed x2, waiting for transfers between devices  119 us
    another operation x8, local copies, waits for them, and re-layouts, shifted_blocks(): jnp.stack([padded[..., TAPS - lag:TAPS - lag + samples] for lag in range(...  41.7 us
    all_to_all x1, waiting for transfers between devices, deliver(): lax.all_to_all(first, ('handler', 'worker'), split_axis=0, concat_axis=0,...  13.5 us
  transfers between devices with their start and end apart: 4, of which 3 were waited for; matrix products, arithmetic and copies ran while one was open for 4% of the time, Pallas kernels for 0%

commit v1 on v0

v1 whole, which is shorter than its diff:
```python
import functools
import jax
import jax.numpy as jnp
from jax import lax
from jax.experimental import pallas as pl
from jax.experimental.pallas import tpu as pltpu
from jax.sharding import PartitionSpec as P

TAPS = 64
BLK = 2
RUP_SLOTS = 4
OUTER = 4
INNER = TAPS // OUTER


def combine_points(sgt, mechanism):
    total = mechanism[0].astype(jnp.float32)[:, None, None] * sgt[:, 0].astype(jnp.float32)
    for comp in range(1, 6):
        total = total + mechanism[comp].astype(jnp.float32)[:, None, None] * sgt[:, comp].astype(
            jnp.float32
        )
    return total.astype(jnp.bfloat16)


def conv_kernel(rows, variations, samples, workers, blk_ref, slip_ref, out_ref, shift_ref):
    depth = INNER * BLK * rows
    share = variations // workers
    lane = lax.broadcasted_iota(jnp.int32, (BLK * rows, samples), 1)
    wide = lax.broadcasted_iota(jnp.int32, (variations, samples), 1)

    def slot_step(slot, carry):
        left = jnp.concatenate(
            [slip_ref[slot, :, a * depth : (a + 1) * depth] for a in range(OUTER)], axis=0
        )
        for k in range(3):
            x = jnp.concatenate(
                [
                    blk_ref[slot, :, (i * 3 + k) * samples : (i * 3 + k + 1) * samples]
                    for i in range(BLK)
                ],
                axis=0,
            ).astype(jnp.float32)
            for b in range(INNER):
                moved = x if b == 0 else jnp.where(lane >= b, pltpu.roll(x, b, 1), 0.0)
                shift_ref[b * BLK * rows : (b + 1) * BLK * rows, :] = moved.astype(jnp.bfloat16)
            y = jnp.dot(left, shift_ref[...], preferred_element_type=jnp.float32)
            total = y[:variations]
            for a in range(1, OUTER):
                part = pltpu.roll(y[a * variations : (a + 1) * variations], a * INNER, 1)
                total = total + jnp.where(wide >= a * INNER, part, 0.0)
            total = total.astype(jnp.bfloat16)
            for w in range(workers):
                out_ref[w, slot, k] = total[w * share : (w + 1) * share]
        return carry

    lax.fori_loop(0, RUP_SLOTS, slot_step, 0)


def local(workers, sgt, mechanism, req_owner, req_local, slip):
    peers = lax.axis_size(("handler", "worker"))
    samples = sgt.shape[-1]
    blocks_here = sgt.shape[0] // BLK
    requests = req_local.shape[0]
    rows = requests // RUP_SLOTS
    variations = slip.shape[1]
    capacity = max(2, (2 * requests + peers - 1) // peers)
    owner = req_owner[:, 0]
    order = jnp.arange(requests)
    same = (owner[:, None] == owner[None, :]) & (order[:, None] > order[None, :])
    position = owner * capacity + jnp.sum(same.astype(jnp.int32), axis=1)
    places = jnp.arange(peers * capacity, dtype=jnp.int32)
    table = jnp.sum(
        jnp.where(position[:, None] == places[None, :], req_local[:, None], 0), axis=0
    )
    asked = lax.all_to_all(
        table.reshape(peers, capacity),
        ("handler", "worker"),
        split_axis=0,
        concat_axis=0,
        tiled=True,
    )
    green_here = combine_points(sgt, mechanism).reshape(blocks_here, BLK * 3 * samples)
    chosen = green_here[asked.reshape(-1)].reshape(peers, capacity * BLK * 3 * samples)
    chosen = chosen.reshape(peers, capacity, BLK * 3 * samples)
    arrived = lax.all_to_all(
        chosen, ("handler", "worker"), split_axis=0, concat_axis=0, tiled=True
    )
    blocks = arrived.reshape(peers * capacity, BLK * 3 * samples)[position]
    blocks = blocks.reshape(RUP_SLOTS, rows, BLK * 3 * samples)

    full = rows * BLK * TAPS
    src = jnp.arange(full, dtype=jnp.int32)
    dst_of = (
        (src % TAPS) * (BLK * rows) + (src // TAPS) % BLK * rows + src // (TAPS * BLK)
    )
    move = (dst_of[:, None] == src[None, :]).astype(jnp.bfloat16)
    flat = jnp.transpose(slip.reshape(RUP_SLOTS, rows, variations, BLK * TAPS), (0, 2, 1, 3))
    flat = flat.reshape(RUP_SLOTS * variations, full)
    left = jnp.dot(flat, move, preferred_element_type=jnp.bfloat16)
    left = left.reshape(RUP_SLOTS, variations, full)

    share = variations // workers
    partial_value = pl.pallas_call(
        functools.partial(conv_kernel, rows, variations, samples, workers),
        out_shape=jax.ShapeDtypeStruct((workers, RUP_SLOTS, 3, share, samples), jnp.bfloat16),
        in_specs=[pl.BlockSpec(memory_space=pltpu.VMEM)] * 2,
        out_specs=pl.BlockSpec(memory_space=pltpu.VMEM),
        scratch_shapes=[pltpu.VMEM((INNER * BLK * rows, samples), jnp.bfloat16)],
        compiler_params=pltpu.CompilerParams(vmem_limit_bytes=40 * 1024 * 1024),
    )(blocks, left)
    swapped = lax.all_to_all(partial_value, "worker", split_axis=0, concat_axis=0, tiled=True)
    total = jnp.sum(swapped.astype(jnp.float32), axis=0)
    return jnp.transpose(total, (0, 2, 1, 3))


def solution(mesh):
    return jax.shard_map(
        functools.partial(local, mesh.shape["worker"]),
        mesh=mesh,
        in_specs=(
            P(("site", "handler", "worker"), None, None, None),
            P(None, ("handler", "worker")),
            P(("site", "handler", "worker"), None),
            P(("site", "handler", "worker")),
            P(("site", "handler", "worker"), None, None),
        ),
        out_specs=P(("site", "handler"), "worker", None, None),
        check_vma=False,
    )
```

time: 507 us -> 122 us (0.24); the launches traced: 500 us -> 122 us
  local copies, waits for them, and re-layouts: 307 us -> 29 us
  waiting for transfers between devices: 141 us -> 19.8 us
  blocking collectives: 0 us -> 39.6 us
  between operations: 14.9 us -> 0.23 us
  Pallas kernels: 0 us -> 7.28 us
  matrix products: 6.58 us -> 1.03 us
    unnamed x260 -> x4, local copies, waits for them, and re-layouts: 235 us -> 0.01 us
    unnamed x2 -> x0, waiting for transfers between devices: 119 us -> none
    another operation x13 -> x1, local copies, waits for them, and re-layouts: 51.7 us -> 1.16 us  [local(): chosen = chosen.reshape(peers, capacity, BLK * 3 * samples)]
    all_to_all x0 -> x1, blocking collectives: none -> 39.6 us  [local(): lax.all_to_all(partial_value, 'worker', split_axis=0, concat_axis=0, tile...]
    mul x0 -> x12, local copies, waits for them, and re-layouts: none -> 10.3 us  [the longest x10 8.53 us: combine_points(): mechanism[comp].astype(jnp.float32)[:, None, None]]
    pallas_call x0 -> x1, Pallas kernels: none -> 7.28 us  [local(): pl.pallas_call(functools.partial(conv_kernel, rows, variations, samples,...]
    dot_general x4 -> x1, matrix products: 6.58 us -> 1.03 us  [local(): left = jnp.dot(flat, move, preferred_element_type=jnp.bfloat16)]
    convert_element_type x5 -> x10, local copies, waits for them, and re-layouts: 9.5 us -> 12.8 us  [combine_points(): sgt[:, comp].astype(jnp.float32)]
  transfers between devices with their start and end apart: 4 -> 2, of which waited for: 3 -> 1; matrix products, arithmetic and copies ran while one was open for 4% -> 27% of each run, Pallas kernels for 0% -> 0%
where the time goes in v1:
time: 122 us
  blocking collectives  39.6 us (32%)
  local copies, waits for them, and re-layouts  29 us (24%)
  waiting for transfers between devices  19.8 us (16%)
  starting transfers between devices  13.4 us (11%)
  other arithmetic  11.3 us (9%)
  Pallas kernels  7.28 us (6%)
    all_to_all x1, blocking collectives, local(): lax.all_to_all(partial_value, 'worker', split_axis=0, concat_axis=0, tile...  39.6 us
    all_to_all x1, waiting for transfers between devices, local(): lax.all_to_all(chosen, ('handler', 'worker'), split_axis=0, concat_axis=0...  19.8 us
    convert_element_type x10, local copies, waits for them, and re-layouts, combine_points(): sgt[:, comp].astype(jnp.float32)  12.8 us
    mul x10, local copies, waits for them, and re-layouts, combine_points(): mechanism[comp].astype(jnp.float32)[:, None, None]  8.53 us
    all_to_all x1, starting transfers between devices, local(): lax.all_to_all(table.reshape(peers, capacity), ('handler', 'worker'), spl...  7.39 us
    pallas_call x1, Pallas kernels, local(): pl.pallas_call(functools.partial(conv_kernel, rows, variations, samples,...  7.28 us
    all_to_all x1, starting transfers between devices, local(): lax.all_to_all(chosen, ('handler', 'worker'), split_axis=0, concat_axis=0...  6 us
    convert_element_type x1, other arithmetic, combine_points(): sgt[:, 0].astype(jnp.float32)  3.63 us
  transfers between devices with their start and end apart: 2, of which 1 were waited for; matrix products, arithmetic and copies ran while one was open for 27% of the time, Pallas kernels for 0%

profile of v1, /device:TPU:0, one launch (start us, length us, event | category | flops | bytes accessed | tf_op | source)
XLA Modules:
  0.0 121.7 jit_solution(1279697789015597306)
XLA Ops:
  0.0 0.9 convert_reduce_fusion.1
  0.9 0.7 fusion.20
  1.6 0.7 select_reduce_fusion
  2.3 0.7 all_to_all.12
  3.0 7.4 %all-to-all-start = ((s32[16,1,4]{2,1,0:T(1,128)}), s32[16,1,4]{2,1,0:T(1,128)S(1)}, u32[]{:S(2)}, u32[]{:S(2)}) async-start(s32[16,1,4]{2,1,0:T(1,128)} %bitcast.9), calls=%async_computation | async-start | bytes 16384 | tf_op jit(solution)/shard_map/all_to_all | solution.py:75
  10.4 3.6 %slice_convert_fusion.5 = (f32[64,1,3,1024]{3,0,2,1:T(8,128)S(1)}, f32[64,1,3,1024]{3,0,2,1:T(8,128)}, f32[64,1,3,1024]{3,0,2,1:T(8,128)}, f32[64,1,3,1024]{3,0,...) fusion(bf16[64,6,3,1024]{3,0,2,1:T(8,128)(2,1)} %param.5), kind=kLoop, calls=%fused_computation.14 | loop fusion | flops 1179648 | bytes 7077888 | tf_op jit(solution)/shard_map/convert_element_type | solution.py:17
  14.0 0.5 copy.27
  14.6 0.6 reshape.172
  15.2 0.5 copy.28
  15.7 0.6 reshape.174
  16.3 1.7 %copy.29 = f32[64,1,3,1024]{3,2,0,1:T(4,128)S(1)} copy(f32[64,1,3,1024]{3,0,2,1:T(8,128)} %get-tuple-element.7) | data formatting | bytes 1572864 | tf_op jit(solution)/shard_map/convert_element_type | solution.py:19
  18.0 0.6 reshape.176
  18.6 1.7 %copy.30 = f32[64,1,3,1024]{3,2,0,1:T(4,128)S(1)} copy(f32[64,1,3,1024]{3,0,2,1:T(8,128)} %get-tuple-element.6) | data formatting | bytes 1572864 | tf_op jit(solution)/shard_map/convert_element_type | solution.py:19
  20.3 1.5 %reshape.178 = f32[32,6144]{1,0:T(8,128)} reshape(f32[64,1,3,1024]{3,2,0,1:T(4,128)S(1)} %copy.30) | data formatting | bytes 1572864 | tf_op jit(solution)/shard_map/convert_element_type | solution.py:19
  21.7 1.7 %copy.31 = f32[64,1,3,1024]{3,2,0,1:T(4,128)S(1)} copy(f32[64,1,3,1024]{3,0,2,1:T(8,128)} %get-tuple-element.10) | data formatting | bytes 1572864 | tf_op jit(solution)/shard_map/convert_element_type | solution.py:19
  23.4 0.0 copy-start.1
  23.4 1.5 %reshape.180 = f32[32,6144]{1,0:T(8,128)} reshape(f32[64,1,3,1024]{3,2,0,1:T(4,128)S(1)} %copy.31) | data formatting | bytes 1572864 | tf_op jit(solution)/shard_map/convert_element_type | solution.py:19
  24.9 1.7 %copy.32 = f32[64,1,3,1024]{3,2,0,1:T(4,128)S(1)} copy(f32[64,1,3,1024]{3,0,2,1:T(8,128)} %get-tuple-element.9) | data formatting | bytes 1572864 | tf_op jit(solution)/shard_map/convert_element_type | solution.py:19
  26.6 1.5 %reshape.182 = f32[32,6144]{1,0:T(8,128)} reshape(f32[64,1,3,1024]{3,2,0,1:T(4,128)S(1)} %copy.32) | data formatting | bytes 1572864 | tf_op jit(solution)/shard_map/convert_element_type | solution.py:19
  28.1 0.2 mul.100
  28.3 1.5 %mul.101 = f32[32,6144]{1,0:T(8,128)} reshape(f32[64,3,1024]{2,1,0:T(4,128)S(1)} %mul.100) | data formatting | bytes 1572864 | tf_op jit(solution)/shard_map/mul | solution.py:19
  29.8 0.2 mul.103
  30.0 1.5 %mul.104 = f32[32,6144]{1,0:T(8,128)} reshape(f32[64,3,1024]{2,1,0:T(4,128)S(1)} %mul.103) | data formatting | bytes 1572864 | tf_op jit(solution)/shard_map/mul | solution.py:19
  31.4 0.2 mul.106
  31.6 1.5 %mul.107 = f32[32,6144]{1,0:T(8,128)} reshape(f32[64,3,1024]{2,1,0:T(4,128)S(1)} %mul.106) | data formatting | bytes 1572864 | tf_op jit(solution)/shard_map/mul | solution.py:19
  33.1 0.2 mul.109
  33.3 1.5 %mul.110 = f32[32,6144]{1,0:T(8,128)} reshape(f32[64,3,1024]{2,1,0:T(4,128)S(1)} %mul.109) | data formatting | bytes 1572864 | tf_op jit(solution)/shard_map/mul | solution.py:19
  34.8 0.2 mul.94
  35.0 1.5 %mul.95 = f32[32,6144]{1,0:T(8,128)} reshape(f32[64,3,1024]{2,1,0:T(4,128)S(1)} %mul.94) | data formatting | bytes 1572864 | tf_op jit(solution)/shard_map/mul | solution.py:17
  36.5 0.2 mul.97
  36.7 1.7 %mul.98 = f32[32,6144]{1,0:T(8,128)} reshape(f32[64,3,1024]{2,1,0:T(4,128)S(1)} %mul.97) | data formatting | bytes 1572864 | tf_op jit(solution)/shard_map/mul | solution.py:19
  38.4 3.5 %add_convert_fusion = bf16[32,6144]{1,0:T(8,128)(2,1)S(1)} fusion(f32[32,6144]{1,0:T(8,128)} %mul.110, f32[32,6144]{1,0:T(8,128)} %reshape.182, f32[32,6144]{1,0:T(8,128)} %mul.107, f32[32,6144]{1,0:T(8,128)} %reshape.180, f32[32,6144]{1,0:T(8,128)} %mul.104, f32[32,6144]{1,0:T(8,128)} %reshape.178, f32[32,6144]{1,0:T(8,128)} %mul.101, ...), kind=kLoop, calls=%fused_computation.6 | loop fusion | flops 2359296 | bytes 9830400 | tf_op jit(solution)/shard_map/convert_element_type | solution.py:22
  41.9 0.0 all-to-all-done
  41.9 0.5 broadcast.142
  42.4 0.7 reduce.3
  43.1 0.1 reshape.165
  43.2 1.0 gather_fusion
  44.2 0.0 copy-start
  44.2 1.2 reshape_reshape.3
  45.4 6.0 %all-to-all-start.1 = ((bf16[16,4,6144]{2,1,0:T(4,128)(2,1)}), bf16[16,4,6144]{2,1,0:T(4,128)(2,1)S(1)}, u32[]{:S(2)}, u32[]{:S(2)}) async-start(bf16[16,4,6144]{2,1,0:T(4,128)(2,1)} %reshape_reshape.3), calls=%async_computation.1 | async-start | bytes 1572864 | tf_op jit(solution)/shard_map/all_to_all | solution.py:85
  51.4 0.3 copy.34
  51.8 1.0 fusion
  52.8 19.8 %all-to-all-done.1 = bf16[16,4,6144]{2,1,0:T(4,128)(2,1)S(1)} async-done(((bf16[16,4,6144]{2,1,0:T(4,128)(2,1)}), bf16[16,4,6144]{2,1,0:T(4,128)(2,1)S(1)}, u32[]{:S(2)}, u32[]{:S(2)}) %all-to-all-start.1) | async-done | bytes 786464 | tf_op jit(solution)/shard_map/all_to_all | solution.py:85
  72.6 0.2 reshape.166
  72.8 0.8 gather_fusion.1
  73.6 7.3 %shard_map.55 = bf16[4,4,3,16,1024]{4,3,2,1,0:T(8,128)(2,1)S(1)} custom-call(bf16[4,8,6144]{2,1,0:T(8,128)(2,1)S(1)} %bitcast.56, bf16[4,64,1024]{2,1,0:T(8,128)(2,1)S(1)} %bitcast.57), custom_call_target="tpu_custom_call" | custom-call | tf_op jit(solution)/shard_map/pallas_call | solution.py:103
  80.9 39.6 %all_to_all.19 = bf16[4,4,3,16,1024]{4,3,2,1,0:T(8,128)(2,1)S(1)} all-to-all(bf16[4,4,3,16,1024]{4,3,2,1,0:T(8,128)(2,1)S(1)} %shard_map.55), channel_id=1, replica_groups=mesh['site'=2,'handler'=4,'worker'=4] {'worker'}, dimensions={0} | all-to-all | bytes 3145728 | tf_op jit(solution)/shard_map/all_to_all | solution.py:111
  120.5 1.2 convert_reduce_fusion
  (7 shorter events, 0.0 us)
Async XLA Ops:
  3.0 38.9 %all-to-all-start = ((s32[16,1,4]{2,1,0:T(1,128)}), s32[16,1,4]{2,1,0:T(1,128)S(1)}, u32[]{:S(2)}, u32[]{:S(2)}) async-start(s32[16,1,4]{2,1,0:T(1,128)} %bitcast.9), calls=%async_computation | async-start | bytes 16384 | tf_op jit(solution)/shard_map/all_to_all | solution.py:75
  23.4 4.7 %copy-start.1 = (bf16[6,64]{1,0:T(8,128)(2,1)S(1)}, bf16[6,64]{1,0:T(8,128)(2,1)}, u32[]{:S(2)}) copy-start(bf16[6,64]{1,0:T(8,128)(2,1)} %param.6) | copy-start | bytes 2308
  44.2 7.2 %copy-start = (bf16[32,64,128]{2,1,0:T(8,128)(2,1)S(1)}, bf16[32,64,128]{2,1,0:T(8,128)(2,1)}, u32[]{:S(2)}) copy-start(bf16[32,64,128]{2,1,0:T(8,128)(2,1)} %param.9) | copy-start | bytes 1572868
  45.4 27.2 %all-to-all-start.1 = ((bf16[16,4,6144]{2,1,0:T(4,128)(2,1)}), bf16[16,4,6144]{2,1,0:T(4,128)(2,1)S(1)}, u32[]{:S(2)}, u32[]{:S(2)}) async-start(bf16[16,4,6144]{2,1,0:T(4,128)(2,1)} %reshape_reshape.3), calls=%async_computation.1 | async-start | bytes 1572864 | tf_op jit(solution)/shard_map/all_to_all | solution.py:85

commit v2 on v1

--- a/solution.py
+++ b/solution.py
@@ -13,13 +13,31 @@
 INNER = TAPS // OUTER
 
 
+def green_kernel(mech_ref, sgt_ref, out_ref):
+    comps, parts, _, samples = sgt_ref.shape
+    for k in range(parts):
+        total = mech_ref[:, 0:1] * sgt_ref[0, k].astype(jnp.float32)
+        for comp in range(1, comps):
+            total = total + mech_ref[:, comp : comp + 1] * sgt_ref[comp, k].astype(jnp.float32)
+        out_ref[:, k * samples : (k + 1) * samples] = total.astype(jnp.bfloat16)
+
+
 def combine_points(sgt, mechanism):
-    total = mechanism[0].astype(jnp.float32)[:, None, None] * sgt[:, 0].astype(jnp.float32)
-    for comp in range(1, 6):
-        total = total + mechanism[comp].astype(jnp.float32)[:, None, None] * sgt[:, comp].astype(
-            jnp.float32
-        )
-    return total.astype(jnp.bfloat16)
+    points, comps, parts, samples = sgt.shape
+    group = min(16, points)
+    return pl.pallas_call(
+        green_kernel,
+        grid=(points // group,),
+        out_shape=jax.ShapeDtypeStruct((points, parts * samples), jnp.bfloat16),
+        in_specs=[
+            pl.BlockSpec((group, comps), lambda g: (g, 0)),
+            pl.BlockSpec((comps, parts, group, samples), lambda g: (0, 0, g, 0)),
+        ],
+        out_specs=pl.BlockSpec((group, parts * samples), lambda g: (g, 0)),
+        cost_estimate=pl.CostEstimate(
+            flops=12 * sgt.size, bytes_accessed=4 * sgt.size, transcendentals=0
+        ),
+    )(mechanism.astype(jnp.float32).T, jnp.transpose(sgt, (1, 2, 0, 3)))
 
 
 def conv_kernel(rows, variations, samples, workers, blk_ref, slip_ref, out_ref, shift_ref):
@@ -33,13 +51,7 @@
             [slip_ref[slot, :, a * depth : (a + 1) * depth] for a in range(OUTER)], axis=0
         )
         for k in range(3):
-            x = jnp.concatenate(
-                [
-                    blk_ref[slot, :, (i * 3 + k) * samples : (i * 3 + k + 1) * samples]
-                    for i in range(BLK)
-                ],
-                axis=0,
-            ).astype(jnp.float32)
+            x = blk_ref[slot, :, k * samples : (k + 1) * samples].astype(jnp.float32)
             for b in range(INNER):
                 moved = x if b == 0 else jnp.where(lane >= b, pltpu.roll(x, b, 1), 0.0)
                 shift_ref[b * BLK * rows : (b + 1) * BLK * rows, :] = moved.astype(jnp.bfloat16)
@@ -59,7 +71,6 @@
 def local(workers, sgt, mechanism, req_owner, req_local, slip):
     peers = lax.axis_size(("handler", "worker"))
     samples = sgt.shape[-1]
-    blocks_here = sgt.shape[0] // BLK
     requests = req_local.shape[0]
     rows = requests // RUP_SLOTS
     variations = slip.shape[1]
@@ -79,14 +90,16 @@
         concat_axis=0,
         tiled=True,
     )
-    green_here = combine_points(sgt, mechanism).reshape(blocks_here, BLK * 3 * samples)
-    chosen = green_here[asked.reshape(-1)].reshape(peers, capacity * BLK * 3 * samples)
-    chosen = chosen.reshape(peers, capacity, BLK * 3 * samples)
+    green_here = combine_points(sgt, mechanism)
+    point = jnp.arange(BLK, dtype=jnp.int32)
+    picked = asked.reshape(-1)[:, None] * BLK + point[None, :]
+    chosen = green_here[picked.reshape(-1)].reshape(peers, capacity * BLK, 3 * samples)
     arrived = lax.all_to_all(
         chosen, ("handler", "worker"), split_axis=0, concat_axis=0, tiled=True
     )
-    blocks = arrived.reshape(peers * capacity, BLK * 3 * samples)[position]
-    blocks = blocks.reshape(RUP_SLOTS, rows, BLK * 3 * samples)
+    taken = position.reshape(RUP_SLOTS, 1, rows) * BLK + point[None, :, None]
+    blocks = arrived.reshape(peers * capacity * BLK, 3 * samples)[taken.reshape(-1)]
+    blocks = blocks.reshape(RUP_SLOTS, BLK * rows, 3 * samples)
 
     full = rows * BLK * TAPS
     src = jnp.arange(full, dtype=jnp.int32)

time: 122 us -> 96.4 us (0.79)
  local copies, waits for them, and re-layouts: 29 us -> 7.53 us
  other arithmetic: 11.3 us -> 3.65 us
  Pallas kernels: 7.28 us -> 11.1 us
    convert_element_type x12 -> x0, local copies, waits for them, and re-layouts: 14 us -> none  [the longest x10 12.8 us: combine_points(): sgt[:, comp].astype(jnp.float32)]
    mul x12 -> x2, local copies, waits for them, and re-layouts: 10.3 us -> 0.17 us  [the longest x1 0.08 us: local(): picked = asked.reshape(-1)[:, None] * BLK + point[None, :]]
    convert_element_type x3 -> x0, other arithmetic: 7.14 us -> none  [the longest x1 3.63 us: combine_points(): sgt[:, 0].astype(jnp.float32)]
    pallas_call x0 -> x1, Pallas kernels: none -> 3.84 us  [combine_points(): pl.pallas_call(green_kernel, grid=(points // group,), out_shape=jax.Shape...]
    gather x2, local copies, waits for them, and re-layouts: 1.8 us -> 4.61 us  [the longest x1 3.82 us: local(): green_here[picked.reshape(-1)].reshape(peers, capacity * BLK, 3 * samples)]
    transpose x0 -> x1, local copies, waits for them, and re-layouts: none -> 1.39 us  [combine_points(): mechanism.astype(jnp.float32)]
  transfers between devices with their start and end apart: 2 -> 2, of which waited for: 1 -> 2; matrix products, arithmetic and copies ran while one was open for 27% -> 3% of each run, Pallas kernels for 0% -> 4%
where the time goes in v2:
time: 96.4 us; the launch traced here: 96 us
  blocking collectives  39.6 us (41%)
  waiting for transfers between devices  20.7 us (21%)
  starting transfers between devices  12.2 us (13%)
  Pallas kernels  11.1 us (12%)
  local copies, waits for them, and re-layouts  7.53 us (8%)
  other arithmetic  3.65 us (4%)
  matrix products  1.03 us (1%)
    all_to_all x1, blocking collectives, local(): lax.all_to_all(partial_value, 'worker', split_axis=0, concat_axis=0, tile...  39.6 us
    all_to_all x1, waiting for transfers between devices, local(): lax.all_to_all(chosen, ('handler', 'worker'), split_axis=0, concat_axis=0...  19.5 us
    all_to_all x1, starting transfers between devices, local(): lax.all_to_all(table.reshape(peers, capacity), ('handler', 'worker'), spl...  7.39 us
    pallas_call x1, Pallas kernels, local(): pl.pallas_call(functools.partial(conv_kernel, rows, variations, samples,...  7.28 us
    all_to_all x1, starting transfers between devices, local(): lax.all_to_all(chosen, ('handler', 'worker'), split_axis=0, concat_axis=0...  4.84 us
    pallas_call x1, Pallas kernels, combine_points(): pl.pallas_call(green_kernel, grid=(points // group,), out_shape=jax.Shape...  3.84 us
    gather x1, local copies, waits for them, and re-layouts, local(): green_here[picked.reshape(-1)].reshape(peers, capacity * BLK, 3 * samples)  3.82 us
  transfers between devices with their start and end apart: 2, of which 2 were waited for; matrix products, arithmetic and copies ran while one was open for 3% of the time, Pallas kernels for 4%

profile of v2, /device:TPU:0, one launch (start us, length us, event | category | flops | bytes accessed | tf_op | source)
XLA Modules:
  0.0 96.0 jit_solution(10673710137025602418)
XLA Ops:
  0.0 0.9 convert_reduce_fusion.1
  0.9 0.7 multiply_reduce_fusion.1
  1.6 0.7 select_reduce_fusion
  2.3 0.7 all_to_all.12
  3.0 7.4 %all-to-all-start = ((s32[16,1,4]{2,1,0:T(1,128)}), s32[16,1,4]{2,1,0:T(1,128)S(1)}, u32[]{:S(2)}, u32[]{:S(2)}) async-start(s32[16,1,4]{2,1,0:T(1,128)} %bitcast.5), calls=%async_computation | async-start | bytes 16384 | tf_op jit(solution)/shard_map/all_to_all | solution.py:86
  10.4 1.4 %copy.12 = f32[6,64]{0,1:T(8,128)} copy(bf16[6,64]{1,0:T(8,128)(2,1)} %param.6) | data formatting | bytes 2304 | tf_op jit(solution)/shard_map/transpose | solution.py:40
  11.8 3.8 %shard_map.55 = bf16[64,3072]{1,0:T(8,128)(2,1)} custom-call(f32[64,6]{1,0:T(8,128)} %bitcast.34, bf16[6,3,64,1024]{3,2,1,0:T(8,128)(2,1)} %bitcast.31), custom_call_target="tpu_custom_call" | custom-call | flops 14155776 | bytes 4718592 | tf_op jit(solution)/shard_map/pallas_call | solution.py:28
  15.7 1.2 %all-to-all-done = s32[16,1,4]{2,1,0:T(1,128)S(1)} async-done(((s32[16,1,4]{2,1,0:T(1,128)}), s32[16,1,4]{2,1,0:T(1,128)S(1)}, u32[]{:S(2)}, u32[]{:S(2)}) %all-to-all-start) | async-done | bytes 288 | tf_op jit(solution)/shard_map/all_to_all | solution.py:86
  16.9 0.1 mul.64
  16.9 0.1 iota_add_fusion
  17.0 0.1 add.131
  17.2 0.0 copy-start
  17.2 3.8 %gather_fusion = bf16[128,3072]{1,0:T(8,128)(2,1)} fusion(bf16[64,3072]{1,0:T(8,128)(2,1)} %shard_map.55, s32[1024]{0:T(1024)S(1)} %pad_clamp_fusion.1), kind=kCustom, calls=%fused_computation | custom fusion | bytes 1573376 | tf_op jit(solution)/shard_map/gather | solution.py:96
  21.0 4.8 %all-to-all-start.1 = ((bf16[16,8,3072]{2,1,0:T(8,128)(2,1)}), bf16[16,8,3072]{2,1,0:T(8,128)(2,1)S(1)}, u32[]{:S(2)}, u32[]{:S(2)}) async-start(bf16[16,8,3072]{2,1,0:T(8,128)(2,1)} %bitcast.7), calls=%async_computation.1 | async-start | bytes 1572864 | tf_op jit(solution)/shard_map/all_to_all | solution.py:97
  25.9 0.1 reduce_sum.34
  26.0 0.1 mul.65
  26.1 0.1 add.138
  26.1 0.0 copy-done
  26.1 0.3 copy.14
  26.5 1.0 %fusion = bf16[1024,256]{0,1:T(8,128)(2,1)S(1)} fusion(s32[1024]{0:T(1024)S(1)} %fusion.14, bf16[32,8,8,128]{3,2,1,0:T(8,128)(2,1)S(1)} %bitcast.33), kind=kOutput, calls=%fused_computation.3 | convolution fusion | flops 537919488 | bytes 1052672 | tf_op jit(solution)/shard_map/dot_general | solution.py:112
  27.6 19.5 %all-to-all-done.1 = bf16[16,8,3072]{2,1,0:T(8,128)(2,1)S(1)} async-done(((bf16[16,8,3072]{2,1,0:T(8,128)(2,1)}), bf16[16,8,3072]{2,1,0:T(8,128)(2,1)S(1)}, u32[]{:S(2)}, u32[]{:S(2)}) %all-to-all-start.1) | async-done | bytes 786464 | tf_op jit(solution)/shard_map/all_to_all | solution.py:97
  47.1 0.8 gather_fusion.1
  47.9 7.3 %shard_map.56 = bf16[4,4,3,16,1024]{4,3,2,1,0:T(8,128)(2,1)S(1)} custom-call(bf16[4,16,3072]{2,1,0:T(8,128)(2,1)S(1)} %bitcast.28, bf16[4,64,1024]{2,1,0:T(8,128)(2,1)S(1)} %bitcast.29), custom_call_target="tpu_custom_call" | custom-call | tf_op jit(solution)/shard_map/pallas_call | solution.py:116
  55.2 39.6 %all_to_all.19 = bf16[4,4,3,16,1024]{4,3,2,1,0:T(8,128)(2,1)S(1)} all-to-all(bf16[4,4,3,16,1024]{4,3,2,1,0:T(8,128)(2,1)S(1)} %shard_map.56), channel_id=1, replica_groups=mesh['site'=2,'handler'=4,'worker'=4] {'worker'}, dimensions={0} | all-to-all | bytes 3145728 | tf_op jit(solution)/shard_map/all_to_all | solution.py:124
  94.8 1.2 %convert_reduce_fusion = f32[4,3,16,1024]{3,2,1,0:T(8,128)} fusion(bf16[4,4,3,16,1024]{4,3,2,1,0:T(8,128)(2,1)S(1)} %all_to_all.19), kind=kLoop, calls=%fused_computation.4 | loop fusion | flops 1376256 | bytes 2359296 | tf_op jit(solution)/shard_map/reduce_sum | solution.py:125
  (8 shorter events, 0.1 us)
Async XLA Ops:
  3.0 13.8 %all-to-all-start = ((s32[16,1,4]{2,1,0:T(1,128)}), s32[16,1,4]{2,1,0:T(1,128)S(1)}, u32[]{:S(2)}, u32[]{:S(2)}) async-start(s32[16,1,4]{2,1,0:T(1,128)} %bitcast.5), calls=%async_computation | async-start | bytes 16384 | tf_op jit(solution)/shard_map/all_to_all | solution.py:86
  17.2 9.0 %copy-start = (bf16[32,64,128]{2,1,0:T(8,128)(2,1)S(1)}, bf16[32,64,128]{2,1,0:T(8,128)(2,1)}, u32[]{:S(2)}) copy-start(bf16[32,64,128]{2,1,0:T(8,128)(2,1)} %param.9) | copy-start | bytes 1572868
  21.0 26.1 %all-to-all-start.1 = ((bf16[16,8,3072]{2,1,0:T(8,128)(2,1)}), bf16[16,8,3072]{2,1,0:T(8,128)(2,1)S(1)}, u32[]{:S(2)}, u32[]{:S(2)}) async-start(bf16[16,8,3072]{2,1,0:T(8,128)(2,1)} %bitcast.7), calls=%async_computation.1 | async-start | bytes 1572864 | tf_op jit(solution)/shard_map/all_to_all | solution.py:97
